TPU v7x, 256 devices: a whole 4x4x8 slice. The times are simulated.
256 devices in a mesh: replica: 8 (over x_lo, y), expert: 16 (over z, core), tensor: 2 (over x_hi).
Axes of the slice: x: 4 (x_hi: 2, x_lo: 2; x = x_hi * 2 + x_lo), y: 4, z: 8, core: 2. Of those that a mesh axis runs over, the one named last changes fastest.
Arguments:
- delta: bfloat16 [8, 256, 16, 14336], P('replica', 'expert', None, 'tensor'), may hold values from -6 to 6
- step_offsets: int32 [8], replicated, may hold values from 0 to 15, as said below
- block_map: int32 [256], replicated, may hold values from 0 to 255, as said below
- master_params: float32 [256, 16, 14336], P('expert', 'replica', 'tensor'), may hold values from -6 to 6
- first_moment: float32 [256, 16, 14336], P('expert', 'replica', 'tensor'), may hold values from -2 to 2
- second_moment: float32 [256, 16, 14336], P('expert', 'replica', 'tensor'), may hold values from 0.01 to 1
Outputs:
- new_params: bfloat16 [256, 16, 14336], P('expert', 'replica')
- new_first: float32 [256, 16, 14336], P('expert', 'replica', 'tensor')
- new_second: float32 [256, 16, 14336], P('expert', 'replica', 'tensor')
Inputs may be any that keep to these rules, and one draw needn't show every extreme that they name: `block_map`: A permutation of the block indices onto owner slots; slot s belongs to expert index s // 16, and the blocks b with b // 16 = i go in equal numbers to every expert index. `step_offsets`: the replica groups' offsets are distinct.
All inputs are finite; a program needn't handle non-finite values.
Results may differ from a plain program's by a relative error of at most 0.0035.
Values may be sent and summed in bfloat16 or wider, within the bound.
A program may use at most 64 MiB of HBM per device.

v0:
```python
import jax
import jax.numpy as jnp
from jax import lax
from jax.sharding import PartitionSpec as P

beta_one = 0.9
beta_two = 0.99
outer_rate = 0.7
outer_round = 20
epsilon = 1e-08


def split_up(value, dim, size):
    before, after = (value.shape[:dim], value.shape[dim + 1 :])
    return jnp.moveaxis(value.reshape(*before, size, -1, *after), dim, 0)


def summed_on_arrival(value, axis, dim):
    blocks = split_up(value, dim, lax.axis_size(axis))
    arrived = lax.all_to_all(blocks, axis, split_axis=0, concat_axis=0, tiled=True)
    return arrived.astype(jnp.float32).sum(axis=0)


def replica_weights(step_offsets):
    reciprocal = 1.0 / (1.0 + step_offsets.astype(jnp.float32))
    return reciprocal / jnp.sum(reciprocal)


def adam_update(gradient, master_params, first_moment, second_moment):
    new_first = beta_one * first_moment + (1.0 - beta_one) * gradient
    new_second = beta_two * second_moment + (1.0 - beta_two) * gradient * gradient
    fix_one = 1.0 - beta_one**outer_round
    fix_two = 1.0 - beta_two**outer_round
    update_step = new_first / fix_one / (jnp.sqrt(new_second / fix_two) + epsilon)
    new_params = (master_params - outer_rate * update_step).astype(jnp.bfloat16)
    return (new_params, new_first, new_second)


def body(delta, step_offsets, block_map, master_params, first_moment, second_moment):
    blocks = delta.shape[1]
    rows_all = delta.shape[2]
    columns = delta.shape[3]
    my_expert = lax.axis_index("expert")
    weights = replica_weights(step_offsets)
    own_weight = weights[lax.axis_index("replica")]
    weighted = (delta[0].astype(jnp.float32) * own_weight).astype(jnp.bfloat16)
    local_map = lax.dynamic_slice_in_dim(block_map, my_expert * blocks, blocks)
    local_ids = jnp.arange(blocks, dtype=jnp.int32)
    sort_order = jnp.argsort(local_map // blocks * blocks + local_ids)
    total_blocks = block_map.shape[0]
    every_id = jnp.arange(total_blocks, dtype=jnp.int32)
    ranked = jnp.where(block_map // blocks == my_expert, every_id, total_blocks + every_id)
    picked = jnp.argsort(ranked)[:blocks]
    placement_ids = jnp.argsort(block_map[picked] % blocks)
    flat_terms = weighted.reshape(blocks, rows_all * columns)
    partial_value = summed_on_arrival(flat_terms, "replica", 1)
    outgoing = partial_value[sort_order]
    arrived = lax.all_to_all(
        outgoing.astype(jnp.bfloat16), "expert", split_axis=0, concat_axis=0, tiled=True
    ).astype(outgoing.dtype)
    summed = arrived[placement_ids]
    gradient = summed.reshape(master_params.shape)
    new_params, new_first, new_second = adam_update(
        gradient, master_params, first_moment, second_moment
    )
    full_params = lax.all_gather(new_params, "tensor", axis=2, tiled=True)
    return (full_params, new_first, new_second)


def solution(mesh):
    in_specs = (
        P("replica", "expert", None, "tensor"),
        P(),
        P(),
        P("expert", "replica", "tensor"),
        P("expert", "replica", "tensor"),
        P("expert", "replica", "tensor"),
    )
    out_specs = (
        P("expert", "replica", None),
        P("expert", "replica", "tensor"),
        P("expert", "replica", "tensor"),
    )
    return jax.shard_map(body, mesh=mesh, in_specs=in_specs, out_specs=out_specs, check_vma=False)
```

profile of v0, /device:TPU:1, one launch (start us, length us, event | category | flops | bytes accessed | tf_op | source)
XLA Modules:
  0.0 123.3 jit_solution(5678902403020369414)
XLA Ops:
  0.6 1.3 %divide_reduce_fusion = f32[]{:T(128)} fusion(s32[8]{0:T(128)} %param.7), kind=kLoop, calls=%fused_computation.33 | loop fusion | flops 31 | bytes 36 | tf_op jit(solution)/shard_map/reduce_sum | solution.py:26
  1.9 1.3 %multiply_divide_fusion = f32[8]{0:T(128)S(1)} fusion(s32[8]{0:T(128)} %param.7, f32[]{:T(128)} %divide_reduce_fusion), kind=kLoop, calls=%fused_computation.32 | loop fusion | flops 32 | bytes 68 | tf_op jit(solution)/shard_map/div | solution.py:26
  3.2 0.6 dynamic_slice.6
  3.8 5.3 %multiply_convert_fusion = bf16[1,16,16,7168]{3,2,1,0:T(8,128)(2,1)} fusion(bf16[1,16,16,7168]{3,2,1,0:T(8,128)(2,1)} %param.6, f32[]{:T(128)} %bitcast), kind=kLoop, calls=%fused_computation.4 | loop fusion | flops 5505024 | bytes 7340036 | tf_op jit(solution)/shard_map/convert_element_type | solution.py:46
  9.1 6.1 %convert_element_type.43 = bf16[16,8,14336]{2,1,0:T(8,128)(2,1)} reshape(bf16[1,16,16,7168]{3,2,1,0:T(8,128)(2,1)} %multiply_convert_fusion) | data formatting | bytes 7340032 | tf_op jit(solution)/shard_map/convert_element_type | solution.py:46
  15.1 5.9 %copy.11 = bf16[8,16,14336]{2,1,0:T(8,128)(2,1)} copy(bf16[8,16,14336]{2,0,1:T(8,128)(2,1)} %bitcast.10) | data formatting | bytes 7340032 | tf_op jit(solution)/shard_map/transpose | solution.py:15
  21.0 6.1 %all-to-all-start = ((bf16[8,16,14336]{2,1,0:T(8,128)(2,1)}), bf16[8,16,14336]{2,1,0:T(8,128)(2,1)}, u32[]{:S(2)}, u32[]{:S(2)}) async-start(bf16[8,16,14336]{2,1,0:T(8,128)(2,1)} %copy.11), calls=%async_computation | async-start | bytes 7340032 | tf_op jit(solution)/shard_map/all_to_all | solution.py:20
  27.2 1.2 %sort.48 = (s32[16]{0:T(128)}, s32[16]{0:T(128)S(1)}) sort(s32[16]{0:T(128)S(1)} %iota_add_fusion, s32[16]{0:T(128)S(1)} %iota.20), dimensions={0}, to_apply=%region_2.3 | sort | flops 64 | bytes 256 | tf_op jit(solution)/shard_map/jit(argsort)/sort | solution.py:49
  28.4 3.2 %sort.49 = (s32[256]{0:T(256)}, s32[256]{0:T(256)S(1)}) sort(s32[256]{0:T(256)S(1)} %compare_select_fusion.5, s32[256]{0:T(256)S(1)} %iota.23), dimensions={0}, to_apply=%region_3.4 | sort | flops 2048 | bytes 4096 | tf_op jit(solution)/shard_map/jit(argsort)/sort | solution.py:53
  31.6 38.6 %all-to-all-done = bf16[8,16,14336]{2,1,0:T(8,128)(2,1)} async-done(((bf16[8,16,14336]{2,1,0:T(8,128)(2,1)}), bf16[8,16,14336]{2,1,0:T(8,128)(2,1)}, u32[]{:S(2)}, u32[]{:S(2)}) %all-to-all-start) | async-done | bytes 3670048 | tf_op jit(solution)/shard_map/all_to_all | solution.py:20
  70.2 2.5 %convert_reduce_fusion = bf16[16,14336]{1,0:T(8,128)(2,1)S(1)} fusion(bf16[8,16,14336]{2,1,0:T(8,128)(2,1)} %all-to-all-done), kind=kLoop, calls=%fused_computation.3 | loop fusion | flops 3440640 | bytes 4128768 | tf_op jit(solution)/shard_map/reduce_sum | solution.py:21
  72.8 0.8 gather_fusion
  73.6 0.5 broadcast.60
  74.1 1.0 reduce
  75.1 1.1 reshape.55
  76.2 9.3 %all-to-all-start.1 = ((bf16[16,2,7168]{2,1,0:T(2,128)(2,1)}), bf16[16,2,7168]{2,1,0:T(2,128)(2,1)S(1)}, u32[]{:S(2)}, u32[]{:S(2)}) async-start(bf16[16,2,7168]{2,1,0:T(2,128)(2,1)} %reshape.55), calls=%async_computation.1 | async-start | bytes 917504 | tf_op jit(solution)/shard_map/all_to_all | solution.py:58
  85.5 0.7 gather_fusion.1
  86.2 1.3 %sort.50 = (s32[16]{0:T(128)}, s32[16]{0:T(128)S(1)}) sort(s32[16]{0:T(128)S(1)} %and_select_fusion, s32[16]{0:T(128)S(1)} %iota.24), dimensions={0}, to_apply=%region_4.5 | sort | flops 64 | bytes 256 | tf_op jit(solution)/shard_map/jit(argsort)/sort | solution.py:54
  87.4 13.9 %all-to-all-done.1 = bf16[16,2,7168]{2,1,0:T(2,128)(2,1)S(1)} async-done(((bf16[16,2,7168]{2,1,0:T(2,128)(2,1)}), bf16[16,2,7168]{2,1,0:T(2,128)(2,1)S(1)}, u32[]{:S(2)}, u32[]{:S(2)}) %all-to-all-start.1) | async-done | bytes 458784 | tf_op jit(solution)/shard_map/all_to_all | solution.py:58
  102.0 0.8 gather_fusion.2
  102.9 0.8 reshape.26
  103.6 4.8 %subtract_convert_fusion = (bf16[16,2,7168]{2,1,0:T(2,128)(2,1)S(1)}, f32[16,2,7168]{2,1,0:T(2,128)}, f32[16,2,7168]{2,1,0:T(2,128)}) fusion(f32[16,2,7168]{2,1,0:T(2,128)S(1)} %copy-done.1, f32[16,2,7168]{2,1,0:T(2,128)S(1)} %reshape.26, f32[16,2,7168]{2,1,0:T(2,128)} %param.10, f32[16,2,7168]{2,1,0:T(2,128)} %param.11), kind=kLoop, calls=%fused_computation.7 | loop fusion | flops 3211264 | bytes 5963776 | tf_op jit(solution)/shard_map/convert_element_type | solution.py:35
  108.5 13.9 %all_gather.3 = bf16[16,2,14336]{2,1,0:T(2,128)(2,1)S(1)} all-gather(bf16[16,2,7168]{2,1,0:T(2,128)(2,1)S(1)} %get-tuple-element.9), channel_id=1, replica_groups=mesh['replica'=8,'expert'=16,'tensor'=2] {'tensor'}, dimensions={2}, use_global_device_ids=true | all-gather | bytes 1376256 | tf_op jit(solution)/shard_map/all_gather | solution.py:66
  122.4 0.9 copy.17
  (18 shorter events, 0.8 us)
Async XLA Ops:
  21.0 6.1 %copy-start = (s32[256]{0:T(256)S(1)}, s32[256]{0:T(256)}, u32[]{:S(2)}) copy-start(s32[256]{0:T(256)} %param.8) | copy-start | bytes 3076
  21.0 49.2 %all-to-all-start = ((bf16[8,16,14336]{2,1,0:T(8,128)(2,1)}), bf16[8,16,14336]{2,1,0:T(8,128)(2,1)}, u32[]{:S(2)}, u32[]{:S(2)}) async-start(bf16[8,16,14336]{2,1,0:T(8,128)(2,1)} %copy.11), calls=%async_computation | async-start | bytes 7340032 | tf_op jit(solution)/shard_map/all_to_all | solution.py:20
  76.2 25.1 %all-to-all-start.1 = ((bf16[16,2,7168]{2,1,0:T(2,128)(2,1)}), bf16[16,2,7168]{2,1,0:T(2,128)(2,1)S(1)}, u32[]{:S(2)}, u32[]{:S(2)}) async-start(bf16[16,2,7168]{2,1,0:T(2,128)(2,1)} %reshape.55), calls=%async_computation.1 | async-start | bytes 917504 | tf_op jit(solution)/shard_map/all_to_all | solution.py:58
  102.0 1.7 %copy-start.1 = (f32[16,2,7168]{2,1,0:T(2,128)S(1)}, f32[16,2,7168]{2,1,0:T(2,128)}, u32[]{:S(2)}) copy-start(f32[16,2,7168]{2,1,0:T(2,128)} %param.9) | copy-start | bytes 2752516
where the time goes:
time: 124 us; the launch traced here: 123 us
  waiting for transfers between devices  52.5 us (42%)
  other arithmetic  22.2 us (18%)
  local copies, waits for them, and re-layouts  18.6 us (15%)
  starting transfers between devices  15.3 us (12%)
  blocking collectives  13.9 us (11%)
    all_to_all x1, waiting for transfers between devices, summed_on_arrival(): lax.all_to_all(blocks, axis, split_axis=0, concat_axis=0, tiled=True)  38.6 us
    all_to_all x1, waiting for transfers between devices, body(): lax.all_to_all(outgoing.astype(jnp.bfloat16), 'expert', split_axis=0, con...  13.9 us
    all_gather x1, blocking collectives, body(): full_params = lax.all_gather(new_params, 'tensor', axis=2, tiled=True)  13.9 us
    all_to_all x1, starting transfers between devices, body(): lax.all_to_all(outgoing.astype(jnp.bfloat16), 'expert', split_axis=0, con...  9.27 us
    all_to_all x1, starting transfers between devices, summed_on_arrival(): lax.all_to_all(blocks, axis, split_axis=0, concat_axis=0, tiled=True)  6.07 us
    convert_element_type x1, local copies, waits for them, and re-layouts, body(): weighted = (delta[0].astype(jnp.float32) * own_weight).astype(jnp.bfloat16)  6.06 us
    transpose x1, local copies, waits for them, and re-layouts, split_up(): return jnp.moveaxis(value.reshape(*before, size, -1, *after), dim, 0)  5.9 us
    convert_element_type x1, other arithmetic, body(): weighted = (delta[0].astype(jnp.float32) * own_weight).astype(jnp.bfloat16)  5.25 us
  transfers between devices with their start and end apart: 2, of which 2 were waited for; matrix products, arithmetic and copies ran while one was open for 5% of the time, Pallas kernels for 0%

commit v1 on v0

v1 whole, which is shorter than its diff:
```python
import functools

import jax
import jax.numpy as jnp
from jax import lax
from jax.experimental import pallas as pl
from jax.experimental.pallas import tpu as pltpu
from jax.sharding import PartitionSpec as P

beta_one = 0.9
beta_two = 0.99
outer_rate = 0.7
outer_round = 20
epsilon = 1e-08

MESH = pl.DeviceIdType.MESH
F32 = jnp.float32
BF16 = jnp.bfloat16

CHUNKS = (1, 1, 1, 1, 1, 1, 1)
LANES = 128
TILES = 8
RING = 4
UNROLL = 4


def adam(gradient, master, first, second):
    new_first = beta_one * first + (1.0 - beta_one) * gradient
    new_second = beta_two * second + (1.0 - beta_two) * gradient * gradient
    fix_one = 1.0 - beta_one**outer_round
    fix_two = 1.0 - beta_two**outer_round
    step = new_first / fix_one / (jnp.sqrt(new_second / fix_two) + epsilon)
    return (master - outer_rate * step).astype(BF16), new_first, new_second


def kernel(experts, blocks, refs):
    chunks = len(CHUNKS)
    starts = [sum(CHUNKS[:k]) for k in range(chunks)]
    (offsets_ref, map_ref, delta_ref, master_ref, first_ref, second_ref) = refs[:6]
    (params_out, first_out, second_out) = refs[6:9]
    scratch = list(refs[9:])

    def take(n):
        got = scratch[:n]
        del scratch[:n]
        return got

    delta_v = take(chunks)
    weighted = take(chunks)
    far = take(chunks)
    passed = take(chunks)
    plain = take(chunks)
    xsend = take(chunks)
    xrecv = take(chunks)
    zsend = take(chunks)
    zrecv = take(chunks)
    master_v = take(chunks)
    first_v = take(chunks)
    second_v = take(chunks)
    params_v = take(chunks)
    (spread, woven) = take(2)
    (order_s, source_s) = take(2)
    (in_sem, out_sem, far_send, far_recv, pass_send, pass_recv, plain_send, plain_recv) = take(8)
    (x_send, x_recv, z_send, z_recv, t_send, t_recv) = take(6)

    replica = lax.axis_index("replica")
    expert = lax.axis_index("expert")
    tensor = lax.axis_index("tensor")
    x = replica // RING
    y = replica % RING
    up = (y + 1) % RING
    down = (y + RING - 1) % RING
    across = (y + 2) % RING
    device_up = {"replica": x * RING + up}
    device_down = {"replica": x * RING + down}
    device_x = {"replica": (1 - x) * RING + y}
    device_t = {"tensor": 1 - tensor}

    barrier = pltpu.get_barrier_semaphore()
    for device in (device_up, device_down, device_x, device_t):
        pl.semaphore_signal(barrier, inc=1, device_id=device, device_id_type=MESH)

    def greet(d, carry):
        pl.semaphore_signal(
            barrier, inc=1, device_id={"expert": (expert + d) % experts}, device_id_type=MESH
        )
        return carry

    lax.fori_loop(1, experts, greet, 0)

    def load_delta(k):
        rows = pl.ds(starts[k] * TILES * 8, CHUNKS[k] * TILES * 8)
        return pltpu.make_async_copy(delta_ref.at[:, :, rows, :], delta_v[k], in_sem.at[k])

    def load_states(k):
        rows = pl.ds(starts[k] * 16, CHUNKS[k] * 16)
        return [
            pltpu.make_async_copy(ref.at[:, rows, :], held[k], in_sem.at[(n + 1) * chunks + k])
            for n, (ref, held) in enumerate(
                ((master_ref, master_v), (first_ref, first_v), (second_ref, second_v))
            )
        ]

    for k in range(chunks):
        load_delta(k).start()
    for k in range(chunks):
        for copy in load_states(k):
            copy.start()

    def find_order(b, held):
        target = lax.shift_right_logical(map_ref[expert * blocks + b], 4)
        return tuple(jnp.where(target == j, b, held[j]) for j in range(experts))

    order = lax.fori_loop(0, blocks, find_order, (jnp.int32(0),) * experts)
    for j in range(experts):
        order_s[j] = order[j]

    def find_source(i, held):
        slot = jnp.int32(0)
        for b in range(blocks):
            offset = map_ref[i * blocks + b] - expert * blocks
            slot = jnp.where((offset >= 0) & (offset < blocks), offset, slot)
        return tuple(jnp.where(slot == s, i, held[s]) for s in range(blocks))

    source = lax.fori_loop(0, experts, find_source, (jnp.int32(0),) * blocks)
    for s in range(blocks):
        source_s[s] = source[s]

    reciprocal = 1.0 / (1.0 + offsets_ref[...].astype(F32))
    weights = reciprocal / jnp.sum(reciprocal, axis=1, keepdims=True)
    lane = lax.broadcasted_iota(jnp.int32, weights.shape, 1)
    weight = jnp.sum(jnp.where(lane == replica, weights, 0.0), axis=1, keepdims=True)

    def remote(src, dst, send, recv, device):
        return pltpu.make_async_remote_copy(
            src_ref=src, dst_ref=dst, send_sem=send, recv_sem=recv, device_id=device, device_id_type=MESH
        )

    def far_copies(k):
        return [
            remote(weighted[k].at[across], far[k].at[0], far_send.at[2 * k], far_recv.at[2 * k], device_up),
            remote(
                weighted[k].at[RING + across], far[k].at[1], far_send.at[2 * k + 1], far_recv.at[2 * k + 1], device_down
            ),
        ]

    def pass_copies(k):
        return [
            remote(far[k].at[0], passed[k].at[0], pass_send.at[2 * k], pass_recv.at[2 * k], device_up),
            remote(far[k].at[1], passed[k].at[1], pass_send.at[2 * k + 1], pass_recv.at[2 * k + 1], device_down),
        ]

    def plain_copies(k):
        return [
            remote(
                weighted[k].at[RING + up], plain[k].at[1], plain_send.at[2 * k], plain_recv.at[2 * k], device_up
            ),
            remote(
                weighted[k].at[down], plain[k].at[0], plain_send.at[2 * k + 1], plain_recv.at[2 * k + 1], device_down
            ),
        ]

    def x_copy(k):
        return remote(xsend[k], xrecv[k], x_send.at[k], x_recv.at[k], device_x)

    def z_copy(k, j):
        return remote(zsend[k].at[j], zrecv[k].at[expert], z_send.at[k], z_recv.at[k], {"expert": j})

    def own_rows(k):
        whole = CHUNKS[k] * 16
        return pl.ds(pl.multiple_of(tensor * (sum(CHUNKS) * 16) + starts[k] * 16, 16), whole)

    def t_copy(k):
        return remote(params_v[k], params_out.at[:, own_rows(k), :], t_send.at[k], t_recv.at[k], device_t)

    def stores(k):
        rows = pl.ds(starts[k] * 16, CHUNKS[k] * 16)
        return [
            pltpu.make_async_copy(params_v[k], params_out.at[:, own_rows(k), :], out_sem.at[k]),
            pltpu.make_async_copy(first_v[k], first_out.at[:, rows, :], out_sem.at[chunks + k]),
            pltpu.make_async_copy(second_v[k], second_out.at[:, rows, :], out_sem.at[2 * chunks + k]),
        ]

    def weigh(k):
        units = CHUNKS[k]
        load_delta(k).wait()

        def some(g, carry):
            for n in range(UNROLL):
                j = g * UNROLL + n
                for h in range(2):
                    spread[n, h, : units * 64, :] = delta_v[k][order_s[j], h].astype(F32) * weight
                for h in range(2):
                    for q in range(RING):
                        for unit in range(units):
                            pair = [
                                spread[n, h, pl.ds(unit * 64 + 2 * q + row, TILES, stride=8), :] for row in range(2)
                            ]
                            weighted[k][RING * h + q, j, unit * 16 : unit * 16 + 16, :] = jnp.concatenate(
                                pair, axis=0
                            ).astype(BF16)
            return carry

        lax.fori_loop(0, experts // UNROLL, some, 0)

    def loop(step):
        def some(g, carry):
            for n in range(UNROLL):
                step(g * UNROLL + n)
            return carry

        lax.fori_loop(0, experts // UNROLL, some, 0)

    def add_on_way(k):
        for copy in far_copies(k):
            copy.wait_recv()

        def step(j):
            for n, place in ((0, up), (1, RING + down)):
                total = far[k][n, j].astype(F32) + weighted[k][place, j].astype(F32)
                far[k][n, j] = total.astype(BF16)

        loop(step)

    def ring_sum(k, h, j):
        total = weighted[k][RING * h + y, j].astype(F32) + plain[k][h, j].astype(F32)
        return total + passed[k][h, j].astype(F32)

    def x_half(k):
        for copy in pass_copies(k) + plain_copies(k):
            copy.wait_recv()

        def step(j):
            xsend[k][j] = ring_sum(k, 1 - x, j).astype(BF16)

        loop(step)
        x_copy(k).start()

    def finish(k):
        x_copy(k).wait_recv()

        def step(j):
            zsend[k][j] = (ring_sum(k, x, j) + xrecv[k][j].astype(F32)).astype(BF16)

        loop(step)

        def send(d, carry):
            z_copy(k, (expert + d) % experts).start()
            return carry

        lax.fori_loop(1, experts, send, 0)
        zrecv[k][expert] = zsend[k][expert]

    def all_of(k, ref, sem):
        return pltpu.make_async_copy(ref.at[: experts - 1], ref.at[: experts - 1], sem.at[k])

    def update(k):
        all_of(k, zrecv[k], z_recv).wait()
        for copy in load_states(k):
            copy.wait()

        def step(s, n):
            arrived = zrecv[k][source_s[s]].astype(F32)
            for unit in range(CHUNKS[k]):
                for row in range(2):
                    woven[n, pl.ds(unit * 16 + row, TILES, stride=2), :] = arrived[
                        unit * 16 + row * 8 : unit * 16 + row * 8 + 8
                    ]
            rows = CHUNKS[k] * 16
            params_v[k][s], first_v[k][s], second_v[k][s] = adam(
                woven[n, :rows], master_v[k][s], first_v[k][s], second_v[k][s]
            )

        def some(g, carry):
            for n in range(UNROLL):
                step(g * UNROLL + n, n)
            return carry

        lax.fori_loop(0, blocks // UNROLL, some, 0)
        t_copy(k).start()
        for copy in stores(k):
            copy.start()

    for t in range(chunks + 4):
        if t < chunks:
            weigh(t)
            if t == 0:
                pl.semaphore_wait(barrier, experts + 3)
            for copy in far_copies(t):
                copy.start()
        if 0 <= t - 1 < chunks:
            add_on_way(t - 1)
            for copy in pass_copies(t - 1):
                copy.start()
        if t < chunks:
            for copy in plain_copies(t):
                copy.start()
        if 0 <= t - 2 < chunks:
            x_half(t - 2)
        if 0 <= t - 3 < chunks:
            finish(t - 3)
        if 0 <= t - 4 < chunks:
            update(t - 4)

    for k in range(chunks):
        for copy in far_copies(k) + pass_copies(k) + plain_copies(k) + [x_copy(k)]:
            copy.wait_send()
        all_of(k, zsend[k], z_send).wait()
        t_copy(k).wait()
        for copy in stores(k):
            copy.wait()


def fused(experts, blocks, *operands):
    chunks = len(CHUNKS)
    units = sum(CHUNKS)
    wide = max(CHUNKS)

    def each(*lead, dtype=BF16):
        return [pltpu.VMEM((*lead, n * 16, LANES), dtype) for n in CHUNKS]

    scratch = [pltpu.VMEM((blocks, 2, n * 64, LANES), BF16) for n in CHUNKS]
    scratch += each(2 * RING, experts)
    scratch += each(2, experts) + each(2, experts) + each(2, experts)
    scratch += each(experts) + each(experts) + each(experts) + each(experts)
    scratch += each(blocks, dtype=F32) + each(blocks, dtype=F32) + each(blocks, dtype=F32) + each(blocks)
    scratch += [pltpu.VMEM((UNROLL, 2, wide * 64, LANES), F32), pltpu.VMEM((UNROLL, wide * 16, LANES), F32)]
    scratch += [pltpu.SMEM((experts,), jnp.int32), pltpu.SMEM((blocks,), jnp.int32)]
    scratch += [pltpu.SemaphoreType.DMA((n * chunks,)) for n in (4, 3, 2, 2, 2, 2, 2, 2, 1, 1, 1, 1, 1, 1)]
    anywhere = pl.BlockSpec(memory_space=pl.ANY)
    return pl.pallas_call(
        lambda *refs: kernel(experts, blocks, refs),
        name="outer_step",
        out_shape=(
            jax.ShapeDtypeStruct((blocks, 2 * units * 16, LANES), BF16),
            jax.ShapeDtypeStruct((blocks, units * 16, LANES), F32),
            jax.ShapeDtypeStruct((blocks, units * 16, LANES), F32),
        ),
        in_specs=[
            pl.BlockSpec(memory_space=pltpu.VMEM),
            pl.BlockSpec(memory_space=pltpu.SMEM),
            anywhere,
            anywhere,
            anywhere,
            anywhere,
        ],
        out_specs=(anywhere, anywhere, anywhere),
        scratch_shapes=scratch,
        compiler_params=pltpu.CompilerParams(
            collective_id=0, has_side_effects=True, vmem_limit_bytes=60 * 1024 * 1024
        ),
    )(*operands)


def tiled(value, rows):
    lead = value.shape[:-2]
    tall, columns = value.shape[-2:]
    split = value.reshape(*lead, tall // rows, rows, columns // LANES, LANES)
    return jnp.swapaxes(split, -3, -2).reshape(*lead, tall // rows, columns // LANES * rows, LANES)


def untiled(value):
    lead, tall, lanes = value.shape
    split = value.reshape(lead, tall // 2, 2, lanes)
    return jnp.swapaxes(split, 1, 2).reshape(lead, 2, tall // 2 * lanes)


def body(experts, delta, step_offsets, block_map, master_params, first_moment, second_moment):
    blocks = master_params.shape[0]
    states = [tiled(value, 2)[:, 0] for value in (master_params, first_moment, second_moment)]
    outs = fused(experts, blocks, step_offsets[None], block_map, tiled(delta[0], 8), *states)
    return tuple(untiled(value) for value in outs)


def solution(mesh):
    in_specs = (
        P("replica", "expert", None, "tensor"),
        P(),
        P(),
        P("expert", "replica", "tensor"),
        P("expert", "replica", "tensor"),
        P("expert", "replica", "tensor"),
    )
    out_specs = (
        P("expert", "replica", None),
        P("expert", "replica", "tensor"),
        P("expert", "replica", "tensor"),
    )
    step = functools.partial(body, mesh.shape["expert"])
    return jax.shard_map(step, mesh=mesh, in_specs=in_specs, out_specs=out_specs, check_vma=False)
```

time: 124 us -> 65.1 us (0.52)
  Pallas kernels: 0 us -> 58.3 us
  waiting for transfers between devices: 52.5 us -> 0 us
  other arithmetic: 22.2 us -> 0 us
  starting transfers between devices: 15.3 us -> 0 us
  blocking collectives: 13.9 us -> 0 us
  local copies, waits for them, and re-layouts: 18.6 us -> 5.9 us
    pallas_call x0 -> x1, Pallas kernels: none -> 58.3 us  [fused(): pl.pallas_call(lambda *refs: kernel(experts, blocks, refs), name='outer_s...]
    all_to_all x2 -> x0, waiting for transfers between devices: 52.5 us -> none  [the longest x1 38.6 us: summed_on_arrival(): lax.all_to_all(blocks, axis, split_axis=0, concat_axis=0, tiled=True)]
    all_to_all x2 -> x0, starting transfers between devices: 15.3 us -> none  [the longest x1 9.27 us: body(): lax.all_to_all(outgoing.astype(jnp.bfloat16), 'expert', split_axis=0, con...]
    all_gather x1 -> x0, blocking collectives: 13.9 us -> none  [body(): full_params = lax.all_gather(new_params, 'tensor', axis=2, tiled=True)]
    convert_element_type x4 -> x0, other arithmetic: 11.3 us -> none  [the longest x1 5.25 us: body(): weighted = (delta[0].astype(jnp.float32) * own_weight).astype(jnp.bfloat16)]
    convert_element_type x2 -> x0, local copies, waits for them, and re-layouts: 6.58 us -> none  [the longest x1 6.06 us: body(): weighted = (delta[0].astype(jnp.float32) * own_weight).astype(jnp.bfloat16)]
    transpose x1 -> x0, local copies, waits for them, and re-layouts: 5.9 us -> none  [split_up(): return jnp.moveaxis(value.reshape(*before, size, -1, *after), dim, 0)]
    sort x3 -> x0, other arithmetic: 5.67 us -> none  [the longest x1 3.17 us: body(): picked = jnp.argsort(ranked)[:blocks]]
  transfers between devices with their start and end apart: 2 -> 0, of which waited for: 2 -> 0; matrix products, arithmetic and copies ran while one was open for 5% -> 0% of each run, Pallas kernels for 0% -> 0%
where the time goes in v1:
time: 65.1 us; the launch traced here: 64.9 us
  Pallas kernels  58.3 us (90%)
  local copies, waits for them, and re-layouts  5.9 us (9%)
    pallas_call x1, Pallas kernels, fused(): pl.pallas_call(lambda *refs: kernel(experts, blocks, refs), name='outer_s...  58.3 us
    unnamed x5, local copies, waits for them, and re-layouts  5.9 us

profile of v1, /device:TPU:1, one launch (start us, length us, event | category | flops | bytes accessed | tf_op | source)
XLA Modules:
  0.0 64.9 jit_solution(16921118138936370069)
XLA Ops:
  0.6 58.3 %outer_step.1 = (bf16[16,224,128]{2,1,0:T(8,128)(2,1)}, f32[16,112,128]{2,1,0:T(8,128)}, f32[16,112,128]{2,1,0:T(8,128)}) custom-call(s32[1,8]{1,0:T(1,128)} %bitcast.43, s32[256]{0:T(256)} %refs_1_.1, bf16[16,2,448,128]{3,2,1,0:T(8,128)(2,1)} %bitcast.36, f32[16,112,128]{2,1,0:T(8,128)} %bitcast.40, f32[16,112,128]{2,1,0:T(8,128)} %bitcast.41, ...), custom_call_target="tpu_custom_call" | custom-call | tf_op jit(solution)/shard_map/outer_step/pallas_call | solution.py:331
  59.0 0.0 copy-start
  59.0 2.8 %copy.18 = bf16[16,2,14336]{2,1,0:T(2,128)(2,1)} copy(bf16[16,2,14336]{2,1,0:T(2,128)(2,1)} %bitcast.39) | data formatting | bytes 1835008
  61.8 2.2 %copy.19 = f32[16,2,7168]{2,1,0:T(2,128)} copy(f32[16,2,7168]{2,1,0:T(2,128)} %bitcast.38) | data formatting | bytes 1835008
  64.0 0.0 copy-done
  64.0 0.9 %copy.20 = f32[16,2,7168]{2,1,0:T(2,128)} copy(f32[16,2,7168]{2,1,0:T(2,128)S(1)} %bitcast.37) | data formatting | bytes 1835008
Async XLA Ops:
  59.0 5.0 %copy-start = (f32[16,112,128]{2,1,0:T(8,128)S(1)}, f32[16,112,128]{2,1,0:T(8,128)}, u32[]{:S(2)}) copy-start(f32[16,112,128]{2,1,0:T(8,128)} %get-tuple-element.8) | copy-start | bytes 2752516

commit v2 on v1

--- a/solution.py
+++ b/solution.py
@@ -18,6 +18,10 @@
 BF16 = jnp.bfloat16
 
 CHUNKS = (1, 1, 1, 1, 1, 1, 1)
+FIRST = "yyyyxxx"
+ORDER = (
+    "W4", "W0", "W1", "L0", "W5", "L1", "P0", "P1", "D4", "L4", "W6", "W2", "X0", "W3", "X1", "P4", "L2", "D5", "P2", "P3", "Z4", "L3", "P5", "D6", "X2", "Z0", "L5", "U4", "L6", "Z1", "X3", "Z2", "P6", "Z5", "U0", "Z3", "Z6", "U1", "U2", "U5", "U3", "U6",
+)
 LANES = 128
 TILES = 8
 RING = 4
@@ -36,7 +40,7 @@
 def kernel(experts, blocks, refs):
     chunks = len(CHUNKS)
     starts = [sum(CHUNKS[:k]) for k in range(chunks)]
-    (offsets_ref, map_ref, delta_ref, master_ref, first_ref, second_ref) = refs[:6]
+    (offsets_hbm, map_hbm, delta_ref, master_ref, first_ref, second_ref) = refs[:6]
     (params_out, first_out, second_out) = refs[6:9]
     scratch = list(refs[9:])
 
@@ -57,10 +61,9 @@
     master_v = take(chunks)
     first_v = take(chunks)
     second_v = take(chunks)
-    params_v = take(chunks)
     (spread, woven) = take(2)
-    (order_s, source_s) = take(2)
-    (in_sem, out_sem, far_send, far_recv, pass_send, pass_recv, plain_send, plain_recv) = take(8)
+    (offsets_ref, map_ref, order_s, source_s) = take(4)
+    (small_sem, in_sem, far_send, far_recv, pass_send, pass_recv, plain_send, plain_recv) = take(8)
     (x_send, x_recv, z_send, z_recv, t_send, t_recv) = take(6)
 
     replica = lax.axis_index("replica")
@@ -101,12 +104,18 @@
             )
         ]
 
+    load_map = pltpu.make_async_copy(map_hbm, map_ref, small_sem.at[0])
+    load_offsets = pltpu.make_async_copy(offsets_hbm, offsets_ref, small_sem.at[1])
+    load_map.start()
+    load_offsets.start()
     for k in range(chunks):
         load_delta(k).start()
     for k in range(chunks):
         for copy in load_states(k):
             copy.start()
 
+    load_map.wait()
+
     def find_order(b, held):
         target = lax.shift_right_logical(map_ref[expert * blocks + b], 4)
         return tuple(jnp.where(target == j, b, held[j]) for j in range(experts))
@@ -115,53 +124,62 @@
     for j in range(experts):
         order_s[j] = order[j]
 
-    def find_source(i, held):
-        slot = jnp.int32(0)
-        for b in range(blocks):
-            offset = map_ref[i * blocks + b] - expert * blocks
-            slot = jnp.where((offset >= 0) & (offset < blocks), offset, slot)
-        return tuple(jnp.where(slot == s, i, held[s]) for s in range(blocks))
-
-    source = lax.fori_loop(0, experts, find_source, (jnp.int32(0),) * blocks)
-    for s in range(blocks):
-        source_s[s] = source[s]
-
+    load_offsets.wait()
     reciprocal = 1.0 / (1.0 + offsets_ref[...].astype(F32))
     weights = reciprocal / jnp.sum(reciprocal, axis=1, keepdims=True)
     lane = lax.broadcasted_iota(jnp.int32, weights.shape, 1)
     weight = jnp.sum(jnp.where(lane == replica, weights, 0.0), axis=1, keepdims=True)
 
+    def find_sources():
+        def find_source(i, held):
+            slot = jnp.int32(0)
+            for b in range(blocks):
+                offset = map_ref[i * blocks + b] - expert * blocks
+                slot = jnp.where((offset >= 0) & (offset < blocks), offset, slot)
+            return tuple(jnp.where(slot == s, i, held[s]) for s in range(blocks))
+
+        source = lax.fori_loop(0, experts, find_source, (jnp.int32(0),) * blocks)
+        for s in range(blocks):
+            source_s[s] = source[s]
+
     def remote(src, dst, send, recv, device):
         return pltpu.make_async_remote_copy(
             src_ref=src, dst_ref=dst, send_sem=send, recv_sem=recv, device_id=device, device_id_type=MESH
         )
 
+    half = experts // 2
+    low, high = pl.ds(0, half), pl.ds(half, half)
+
+    def both_ways(k, up_from, up_to, down_from, down_to, send, recv):
+        return [
+            remote(up_from, up_to, send.at[2 * k], recv.at[2 * k], device_up),
+            remote(down_from, down_to, send.at[2 * k + 1], recv.at[2 * k + 1], device_down),
+        ]
+
     def far_copies(k):
-        return [
-            remote(weighted[k].at[across], far[k].at[0], far_send.at[2 * k], far_recv.at[2 * k], device_up),
-            remote(
-                weighted[k].at[RING + across], far[k].at[1], far_send.at[2 * k + 1], far_recv.at[2 * k + 1], device_down
-            ),
-        ]
+        if FIRST[k] == "y":
+            ends = (weighted[k].at[across], far[k].at[0], weighted[k].at[RING + across], far[k].at[1])
+        else:
+            ends = (xsend[k].at[across, low], far[k].at[low], xsend[k].at[across, high], far[k].at[high])
+        return both_ways(k, *ends, far_send, far_recv)
 
     def pass_copies(k):
-        return [
-            remote(far[k].at[0], passed[k].at[0], pass_send.at[2 * k], pass_recv.at[2 * k], device_up),
-            remote(far[k].at[1], passed[k].at[1], pass_send.at[2 * k + 1], pass_recv.at[2 * k + 1], device_down),
-        ]
+        if FIRST[k] == "y":
+            ends = (far[k].at[0], passed[k].at[0], far[k].at[1], passed[k].at[1])
+        else:
+            ends = (far[k].at[low], passed[k].at[low], far[k].at[high], passed[k].at[high])
+        return both_ways(k, *ends, pass_send, pass_recv)
 
     def plain_copies(k):
-        return [
-            remote(
-                weighted[k].at[RING + up], plain[k].at[1], plain_send.at[2 * k], plain_recv.at[2 * k], device_up
-            ),
-            remote(
-                weighted[k].at[down], plain[k].at[0], plain_send.at[2 * k + 1], plain_recv.at[2 * k + 1], device_down
-            ),
-        ]
+        if FIRST[k] == "y":
+            ends = (weighted[k].at[RING + up], plain[k].at[1], weighted[k].at[down], plain[k].at[0])
+        else:
+            ends = (xsend[k].at[up, high], plain[k].at[high], xsend[k].at[down, low], plain[k].at[low])
+        return both_ways(k, *ends, plain_send, plain_recv)
 
     def x_copy(k):
-        return remote(xsend[k], xrecv[k], x_send.at[k], x_recv.at[k], device_x)
+        source = xsend[k] if FIRST[k] == "y" else weighted[k].at[pl.ds(RING * (1 - x), RING)]
+        return remote(source, xrecv[k], x_send.at[k], x_recv.at[k], device_x)
 
     def z_copy(k, j):
         return remote(zsend[k].at[j], zrecv[k].at[expert], z_send.at[k], z_recv.at[k], {"expert": j})
@@ -171,15 +189,7 @@
         return pl.ds(pl.multiple_of(tensor * (sum(CHUNKS) * 16) + starts[k] * 16, 16), whole)
 
     def t_copy(k):
-        return remote(params_v[k], params_out.at[:, own_rows(k), :], t_send.at[k], t_recv.at[k], device_t)
-
-    def stores(k):
-        rows = pl.ds(starts[k] * 16, CHUNKS[k] * 16)
-        return [
-            pltpu.make_async_copy(params_v[k], params_out.at[:, own_rows(k), :], out_sem.at[k]),
-            pltpu.make_async_copy(first_v[k], first_out.at[:, rows, :], out_sem.at[chunks + k]),
-            pltpu.make_async_copy(second_v[k], second_out.at[:, rows, :], out_sem.at[2 * chunks + k]),
-        ]
+        return remote(params_out.at[:, own_rows(k), :], params_out.at[:, own_rows(k), :], t_send.at[k], t_recv.at[k], device_t)
 
     def weigh(k):
         units = CHUNKS[k]
@@ -211,6 +221,16 @@
 
         lax.fori_loop(0, experts // UNROLL, some, 0)
 
+    def add_x(k):
+        x_copy(k).wait_recv()
+
+        def step(j):
+            for q in range(RING):
+                total = weighted[k][RING * x + q, j].astype(F32) + xrecv[k][q, j].astype(F32)
+                xsend[k][q, j] = total.astype(BF16)
+
+        loop(step)
+
     def add_on_way(k):
         for copy in far_copies(k):
             copy.wait_recv()
@@ -220,35 +240,59 @@
                 total = far[k][n, j].astype(F32) + weighted[k][place, j].astype(F32)
                 far[k][n, j] = total.astype(BF16)
 
-        loop(step)
+        def step_half(g, carry):
+            for n in range(2):
+                for base, place in ((0, up), (half, down)):
+                    j = base + g * 2 + n
+                    far[k][j] = (far[k][j].astype(F32) + xsend[k][place, j].astype(F32)).astype(BF16)
+            return carry
+
+        if FIRST[k] == "y":
+            loop(step)
+        else:
+            lax.fori_loop(0, half // 2, step_half, 0)
 
     def ring_sum(k, h, j):
-        total = weighted[k][RING * h + y, j].astype(F32) + plain[k][h, j].astype(F32)
-        return total + passed[k][h, j].astype(F32)
-
-    def x_half(k):
+        if FIRST[k] == "y":
+            terms = (weighted[k].at[RING * h + y], plain[k].at[h], passed[k].at[h])
+        else:
+            terms = (xsend[k].at[y], plain[k], passed[k])
+        return terms[0][j].astype(F32) + terms[1][j].astype(F32) + terms[2][j].astype(F32)
+
+    def wait_ring(k):
         for copy in pass_copies(k) + plain_copies(k):
             copy.wait_recv()
 
+    def x_half(k):
+        wait_ring(k)
+
         def step(j):
             xsend[k][j] = ring_sum(k, 1 - x, j).astype(BF16)
 
         loop(step)
-        x_copy(k).start()
 
     def finish(k):
-        x_copy(k).wait_recv()
+        if FIRST[k] == "y":
+            x_copy(k).wait_recv()
+        else:
+            wait_ring(k)
 
         def step(j):
-            zsend[k][j] = (ring_sum(k, x, j) + xrecv[k][j].astype(F32)).astype(BF16)
+            total = ring_sum(k, x, j)
+            if FIRST[k] == "y":
+                total = total + xrecv[k][j].astype(F32)
+            zsend[k][j] = total.astype(BF16)
 
         loop(step)
 
-        def send(d, carry):
-            z_copy(k, (expert + d) % experts).start()
+        def send(i, carry):
+            turn = i // 2
+            hops = (turn + 1) // 2 * (1 - 2 * (turn % 2))
+            z = (expert // 2 + experts // 4 + hops + experts) % (experts // 2)
+            z_copy(k, 2 * z + (expert + 1 + i) % 2).start()
             return carry
 
-        lax.fori_loop(1, experts, send, 0)
+        lax.fori_loop(0, experts - 1, send, 0)
         zrecv[k][expert] = zsend[k][expert]
 
     def all_of(k, ref, sem):
@@ -267,9 +311,10 @@
                         unit * 16 + row * 8 : unit * 16 + row * 8 + 8
                     ]
             rows = CHUNKS[k] * 16
-            params_v[k][s], first_v[k][s], second_v[k][s] = adam(
-                woven[n, :rows], master_v[k][s], first_v[k][s], second_v[k][s]
-            )
+            (params, first, second) = adam(woven[n, :rows], master_v[k][s], first_v[k][s], second_v[k][s])
+            params_out[s, own_rows(k), :] = params
+            first_out[s, pl.ds(starts[k] * 16, rows), :] = first
+            second_out[s, pl.ds(starts[k] * 16, rows), :] = second
 
         def some(g, carry):
             for n in range(UNROLL):
@@ -277,38 +322,41 @@
             return carry
 
         lax.fori_loop(0, blocks // UNROLL, some, 0)
-        t_copy(k).start()
-        for copy in stores(k):
+
+    for n, (stage, number) in enumerate(ORDER):
+        k = int(number)
+        copies = []
+        if stage == "W":
+            weigh(k)
+            copies = far_copies(k) if FIRST[k] == "y" else [x_copy(k)]
+        elif stage == "D":
+            add_x(k)
+            copies = far_copies(k)
+        elif stage == "P":
+            add_on_way(k)
+            copies = pass_copies(k)
+        elif stage == "L":
+            copies = plain_copies(k)
+        elif stage == "X" and FIRST[k] == "y":
+            x_half(k)
+            copies = [x_copy(k)]
+        elif stage == "Z":
+            finish(k)
+        elif stage == "U":
+            update(k)
+            copies = [t_copy(k)]
+        if n == 0:
+            pl.semaphore_wait(barrier, experts + 3)
+        for copy in copies:
             copy.start()
-
-    for t in range(chunks + 4):
-        if t < chunks:
-            weigh(t)
-            if t == 0:
-                pl.semaphore_wait(barrier, experts + 3)
-            for copy in far_copies(t):
-                copy.start()
-        if 0 <= t - 1 < chunks:
-            add_on_way(t - 1)
-            for copy in pass_copies(t - 1):
-                copy.start()
-        if t < chunks:
-            for copy in plain_copies(t):
-                copy.start()
-        if 0 <= t - 2 < chunks:
-            x_half(t - 2)
-        if 0 <= t - 3 < chunks:
-            finish(t - 3)
-        if 0 <= t - 4 < chunks:
-            update(t - 4)
+        if n == 0:
+            find_sources()
 
     for k in range(chunks):
         for copy in far_copies(k) + pass_copies(k) + plain_copies(k) + [x_copy(k)]:
             copy.wait_send()
         all_of(k, zsend[k], z_send).wait()
         t_copy(k).wait()
-        for copy in stores(k):
-            copy.wait()
 
 
 def fused(experts, blocks, *operands):
@@ -320,36 +368,38 @@
         return [pltpu.VMEM((*lead, n * 16, LANES), dtype) for n in CHUNKS]
 
     scratch = [pltpu.VMEM((blocks, 2, n * 64, LANES), BF16) for n in CHUNKS]
+    def by_order(first, then):
+        return [
+            pltpu.VMEM((*(first if way == "y" else then), n * 16, LANES), BF16) for n, way in zip(CHUNKS, FIRST)
+        ]
+
     scratch += each(2 * RING, experts)
-    scratch += each(2, experts) + each(2, experts) + each(2, experts)
-    scratch += each(experts) + each(experts) + each(experts) + each(experts)
-    scratch += each(blocks, dtype=F32) + each(blocks, dtype=F32) + each(blocks, dtype=F32) + each(blocks)
+    for _ in range(3):
+        scratch += by_order((2, experts), (experts,))
+    for _ in range(2):
+        scratch += by_order((experts,), (RING, experts))
+    scratch += each(experts) + each(experts)
+    scratch += each(blocks, dtype=F32) + each(blocks, dtype=F32) + each(blocks, dtype=F32)
     scratch += [pltpu.VMEM((UNROLL, 2, wide * 64, LANES), F32), pltpu.VMEM((UNROLL, wide * 16, LANES), F32)]
+    scratch += [pltpu.VMEM(operands[0].shape, jnp.int32), pltpu.SMEM(operands[1].shape, jnp.int32)]
     scratch += [pltpu.SMEM((experts,), jnp.int32), pltpu.SMEM((blocks,), jnp.int32)]
-    scratch += [pltpu.SemaphoreType.DMA((n * chunks,)) for n in (4, 3, 2, 2, 2, 2, 2, 2, 1, 1, 1, 1, 1, 1)]
-    anywhere = pl.BlockSpec(memory_space=pl.ANY)
+    scratch += [pltpu.SemaphoreType.DMA((n,)) for n in (2,)]
+    scratch += [pltpu.SemaphoreType.DMA((n * chunks,)) for n in (4, 2, 2, 2, 2, 2, 2, 1, 1, 1, 1, 1, 1)]
     return pl.pallas_call(
         lambda *refs: kernel(experts, blocks, refs),
         name="outer_step",
         out_shape=(
-            jax.ShapeDtypeStruct((blocks, 2 * units * 16, LANES), BF16),
-            jax.ShapeDtypeStruct((blocks, units * 16, LANES), F32),
-            jax.ShapeDtypeStruct((blocks, units * 16, LANES), F32),
+            pltpu.VMEM((blocks, 2 * units * 16, LANES), BF16),
+            pltpu.VMEM((blocks, units * 16, LANES), F32),
+            pltpu.VMEM((blocks, units * 16, LANES), F32),
         ),
-        in_specs=[
-            pl.BlockSpec(memory_space=pltpu.VMEM),
-            pl.BlockSpec(memory_space=pltpu.SMEM),
-            anywhere,
-            anywhere,
-            anywhere,
-            anywhere,
-        ],
-        out_specs=(anywhere, anywhere, anywhere),
+        in_specs=[pl.BlockSpec(memory_space=pltpu.HBM)] * len(operands),
+        out_specs=(pl.BlockSpec(memory_space=pltpu.VMEM),) * 3,
         scratch_shapes=scratch,
         compiler_params=pltpu.CompilerParams(
-            collective_id=0, has_side_effects=True, vmem_limit_bytes=60 * 1024 * 1024
+            collective_id=0, has_side_effects=True, vmem_limit_bytes=32 * 1024 * 1024
         ),
-    )(*operands)
+    )(*(pltpu.with_memory_space_constraint(value, pltpu.HBM) for value in operands))
 
 
 def tiled(value, rows):

time: 65.1 us -> 54.4 us (0.84)
  Pallas kernels: 58.3 us -> 50.9 us
  local copies, waits for them, and re-layouts: 5.9 us -> 2.77 us
    pallas_call x1, Pallas kernels: 58.3 us -> 50.9 us  [fused(): pl.pallas_call(lambda *refs: kernel(experts, blocks, refs), name='outer_s...]
    unnamed x5 -> x3, local copies, waits for them, and re-layouts: 5.9 us -> 2.77 us
where the time goes in v2:
time: 54.4 us; the launch traced here: 54.3 us
  Pallas kernels  50.9 us (94%)
  local copies, waits for them, and re-layouts  2.77 us (5%)
  between operations  0.64 us (1%)
    pallas_call x1, Pallas kernels, fused(): pl.pallas_call(lambda *refs: kernel(experts, blocks, refs), name='outer_s...  50.9 us
    unnamed x3, local copies, waits for them, and re-layouts  2.77 us

profile of v2, /device:TPU:1, one launch (start us, length us, event | category | flops | bytes accessed | tf_op | source)
XLA Modules:
  0.0 54.3 jit_solution(16714663953311788315)
XLA Ops:
  0.6 50.9 %outer_step.1 = (bf16[16,224,128]{2,1,0:T(8,128)(2,1)S(1)}, f32[16,112,128]{2,1,0:T(8,128)S(1)}, f32[16,112,128]{2,1,0:T(8,128)S(1)}) custom-call(s32[1,8]{1,0:T(1,128)} %bitcast.43, s32[256]{0:T(256)} %refs_1_.1, bf16[16,2,448,128]{3,2,1,0:T(8,128)(2,1)} %bitcast.39, f32[16,112,128]{2,1,0:T(8,128)} %bitcast.40, f32[16,112,128]{2,1,0:T(8,128)} %bitcast.41, ...), custom_call_target="tpu_custom_call" | custom-call | tf_op jit(solution)/shard_map/outer_step/pallas_call | solution.py:388
  51.6 0.9 %copy.18 = bf16[16,2,14336]{2,1,0:T(2,128)(2,1)} copy(bf16[16,2,14336]{2,1,0:T(2,128)(2,1)S(1)} %bitcast.38) | data formatting | bytes 1835008
  52.5 0.9 %copy.19 = f32[16,2,7168]{2,1,0:T(2,128)} copy(f32[16,2,7168]{2,1,0:T(2,128)S(1)} %bitcast.37) | data formatting | bytes 1835008
  53.4 0.9 %copy.20 = f32[16,2,7168]{2,1,0:T(2,128)} copy(f32[16,2,7168]{2,1,0:T(2,128)S(1)} %bitcast.36) | data formatting | bytes 1835008

commit v3 on v2

--- a/solution.py
+++ b/solution.py
@@ -18,9 +18,9 @@
 BF16 = jnp.bfloat16
 
 CHUNKS = (1, 1, 1, 1, 1, 1, 1)
-FIRST = "yyyyxxx"
+FIRST = "yyyyxxz"
 ORDER = (
-    "W4", "W0", "W1", "L0", "W5", "L1", "P0", "P1", "D4", "L4", "W6", "W2", "X0", "W3", "X1", "P4", "L2", "D5", "P2", "P3", "Z4", "L3", "P5", "D6", "X2", "Z0", "L5", "U4", "L6", "Z1", "X3", "Z2", "P6", "Z5", "U0", "Z3", "Z6", "U1", "U2", "U5", "U3", "U6",
+    "W6", "W3", "W2", "W0", "L2", "L0", "S0", "W4", "P2", "W1", "L3", "P0", "P3", "D6", "X2", "W5", "D4", "P1", "Z2", "L4", "P4", "L1", "X0", "E6", "X3", "Z4", "D5", "X1", "L5", "Z0", "L6", "P6", "Z3", "P5", "U2", "Z1", "U6", "U4", "Z5", "U0", "U3", "U1", "U5",
 )
 LANES = 128
 TILES = 8
@@ -114,28 +114,29 @@
         for copy in load_states(k):
             copy.start()
 
-    load_map.wait()
-
-    def find_order(b, held):
-        target = lax.shift_right_logical(map_ref[expert * blocks + b], 4)
-        return tuple(jnp.where(target == j, b, held[j]) for j in range(experts))
-
-    order = lax.fori_loop(0, blocks, find_order, (jnp.int32(0),) * experts)
-    for j in range(experts):
-        order_s[j] = order[j]
-
     load_offsets.wait()
     reciprocal = 1.0 / (1.0 + offsets_ref[...].astype(F32))
     weights = reciprocal / jnp.sum(reciprocal, axis=1, keepdims=True)
     lane = lax.broadcasted_iota(jnp.int32, weights.shape, 1)
     weight = jnp.sum(jnp.where(lane == replica, weights, 0.0), axis=1, keepdims=True)
 
-    def find_sources():
+    def look_up():
+        load_map.wait()
+
+        def find_order(b, held):
+            target = lax.shift_right_logical(map_ref[expert * blocks + b], 4)
+            return tuple(jnp.where(target == j, b, held[j]) for j in range(experts))
+
+        order = lax.fori_loop(0, blocks, find_order, (jnp.int32(0),) * experts)
+        for j in range(experts):
+            order_s[j] = order[j]
+
         def find_source(i, held):
             slot = jnp.int32(0)
             for b in range(blocks):
-                offset = map_ref[i * blocks + b] - expert * blocks
-                slot = jnp.where((offset >= 0) & (offset < blocks), offset, slot)
+                owner = map_ref[i * blocks + b]
+                slot = jnp.where(lax.shift_right_logical(owner, 4) == expert, owner, slot)
+            slot = slot - expert * blocks
             return tuple(jnp.where(slot == s, i, held[s]) for s in range(blocks))
 
         source = lax.fori_loop(0, experts, find_source, (jnp.int32(0),) * blocks)
@@ -156,11 +157,14 @@
             remote(down_from, down_to, send.at[2 * k + 1], recv.at[2 * k + 1], device_down),
         ]
 
+    def y_term(k, place, rows):
+        return xsend[k].at[place, rows] if FIRST[k] == "x" else zrecv[k].at[rows, place]
+
     def far_copies(k):
         if FIRST[k] == "y":
             ends = (weighted[k].at[across], far[k].at[0], weighted[k].at[RING + across], far[k].at[1])
         else:
-            ends = (xsend[k].at[across, low], far[k].at[low], xsend[k].at[across, high], far[k].at[high])
+            ends = (y_term(k, across, low), far[k].at[low], y_term(k, across, high), far[k].at[high])
         return both_ways(k, *ends, far_send, far_recv)
 
     def pass_copies(k):
@@ -174,7 +178,7 @@
         if FIRST[k] == "y":
             ends = (weighted[k].at[RING + up], plain[k].at[1], weighted[k].at[down], plain[k].at[0])
         else:
-            ends = (xsend[k].at[up, high], plain[k].at[high], xsend[k].at[down, low], plain[k].at[low])
+            ends = (y_term(k, up, high), plain[k].at[high], y_term(k, down, low), plain[k].at[low])
         return both_ways(k, *ends, plain_send, plain_recv)
 
     def x_copy(k):
@@ -199,7 +203,7 @@
             for n in range(UNROLL):
                 j = g * UNROLL + n
                 for h in range(2):
-                    spread[n, h, : units * 64, :] = delta_v[k][order_s[j], h].astype(F32) * weight
+                    spread[n, h, : units * 64, :] = delta_v[k][j, h].astype(F32) * weight
                 for h in range(2):
                     for q in range(RING):
                         for unit in range(units):
@@ -224,10 +228,15 @@
     def add_x(k):
         x_copy(k).wait_recv()
 
+        def x_sum(q, j):
+            return (weighted[k][RING * x + q, j].astype(F32) + xrecv[k][q, j].astype(F32)).astype(BF16)
+
         def step(j):
             for q in range(RING):
-                total = weighted[k][RING * x + q, j].astype(F32) + xrecv[k][q, j].astype(F32)
-                xsend[k][q, j] = total.astype(BF16)
+                if FIRST[k] == "x":
+                    xsend[k][q, j] = x_sum(q, j)
+                else:
+                    zsend[k][j, q] = x_sum(q, order_s[j])
 
         loop(step)
 
@@ -244,7 +253,8 @@
             for n in range(2):
                 for base, place in ((0, up), (half, down)):
                     j = base + g * 2 + n
-                    far[k][j] = (far[k][j].astype(F32) + xsend[k][place, j].astype(F32)).astype(BF16)
+                    own = xsend[k][place, j] if FIRST[k] == "x" else zrecv[k][j, place]
+                    far[k][j] = (far[k][j].astype(F32) + own.astype(F32)).astype(BF16)
             return carry
 
         if FIRST[k] == "y":
@@ -254,10 +264,12 @@
 
     def ring_sum(k, h, j):
         if FIRST[k] == "y":
-            terms = (weighted[k].at[RING * h + y], plain[k].at[h], passed[k].at[h])
-        else:
-            terms = (xsend[k].at[y], plain[k], passed[k])
-        return terms[0][j].astype(F32) + terms[1][j].astype(F32) + terms[2][j].astype(F32)
+            terms = (weighted[k][RING * h + y, j], plain[k][h, j], passed[k][h, j])
+        elif FIRST[k] == "x":
+            terms = (xsend[k][y, j], plain[k][j], passed[k][j])
+        else:
+            terms = (zrecv[k][j, y], plain[k][j], passed[k][j])
+        return terms[0].astype(F32) + terms[1].astype(F32) + terms[2].astype(F32)
 
     def wait_ring(k):
         for copy in pass_copies(k) + plain_copies(k):
@@ -278,13 +290,15 @@
             wait_ring(k)
 
         def step(j):
-            total = ring_sum(k, x, j)
+            block = order_s[j]
+            total = ring_sum(k, x, block)
             if FIRST[k] == "y":
-                total = total + xrecv[k][j].astype(F32)
+                total = total + xrecv[k][block].astype(F32)
             zsend[k][j] = total.astype(BF16)
 
         loop(step)
 
+    def to_owners(k):
         def send(i, carry):
             turn = i // 2
             hops = (turn + 1) // 2 * (1 - 2 * (turn % 2))
@@ -299,12 +313,16 @@
         return pltpu.make_async_copy(ref.at[: experts - 1], ref.at[: experts - 1], sem.at[k])
 
     def update(k):
-        all_of(k, zrecv[k], z_recv).wait()
+        if FIRST[k] == "z":
+            wait_ring(k)
+        else:
+            all_of(k, zrecv[k], z_recv).wait()
         for copy in load_states(k):
             copy.wait()
 
         def step(s, n):
-            arrived = zrecv[k][source_s[s]].astype(F32)
+            source = source_s[s]
+            arrived = ring_sum(k, x, source) if FIRST[k] == "z" else zrecv[k][source].astype(F32)
             for unit in range(CHUNKS[k]):
                 for row in range(2):
                     woven[n, pl.ds(unit * 16 + row, TILES, stride=2), :] = arrived[
@@ -326,11 +344,19 @@
     for n, (stage, number) in enumerate(ORDER):
         k = int(number)
         copies = []
-        if stage == "W":
+        if stage == "S":
+            look_up()
+        elif stage == "W":
             weigh(k)
             copies = far_copies(k) if FIRST[k] == "y" else [x_copy(k)]
         elif stage == "D":
             add_x(k)
+            if FIRST[k] == "x":
+                copies = far_copies(k)
+            else:
+                to_owners(k)
+        elif stage == "E":
+            all_of(k, zrecv[k], z_recv).wait()
             copies = far_copies(k)
         elif stage == "P":
             add_on_way(k)
@@ -342,6 +368,7 @@
             copies = [x_copy(k)]
         elif stage == "Z":
             finish(k)
+            to_owners(k)
         elif stage == "U":
             update(k)
             copies = [t_copy(k)]
@@ -349,8 +376,6 @@
             pl.semaphore_wait(barrier, experts + 3)
         for copy in copies:
             copy.start()
-        if n == 0:
-            find_sources()
 
     for k in range(chunks):
         for copy in far_copies(k) + pass_copies(k) + plain_copies(k) + [x_copy(k)]:
@@ -378,7 +403,11 @@
         scratch += by_order((2, experts), (experts,))
     for _ in range(2):
         scratch += by_order((experts,), (RING, experts))
-    scratch += each(experts) + each(experts)
+    for _ in range(2):
+        scratch += [
+            pltpu.VMEM((experts, *((RING,) if way == "z" else ()), n * 16, LANES), BF16)
+            for n, way in zip(CHUNKS, FIRST)
+        ]
     scratch += each(blocks, dtype=F32) + each(blocks, dtype=F32) + each(blocks, dtype=F32)
     scratch += [pltpu.VMEM((UNROLL, 2, wide * 64, LANES), F32), pltpu.VMEM((UNROLL, wide * 16, LANES), F32)]
     scratch += [pltpu.VMEM(operands[0].shape, jnp.int32), pltpu.SMEM(operands[1].shape, jnp.int32)]
@@ -402,6 +431,28 @@
     )(*(pltpu.with_memory_space_constraint(value, pltpu.HBM) for value in operands))
 
 
+def store(*refs):
+    count = len(refs) // 2
+    sem = refs[-1]
+    copies = [pltpu.make_async_copy(refs[n], refs[count + n], sem.at[n]) for n in range(count)]
+    for copy in copies:
+        copy.start()
+    for copy in copies:
+        copy.wait()
+
+
+def stored(*values):
+    return pl.pallas_call(
+        store,
+        name="store",
+        out_shape=tuple(jax.ShapeDtypeStruct(value.shape, value.dtype) for value in values),
+        in_specs=[pl.BlockSpec(memory_space=pltpu.VMEM)] * len(values),
+        out_specs=(pl.BlockSpec(memory_space=pltpu.HBM),) * len(values),
+        scratch_shapes=[pltpu.SemaphoreType.DMA((len(values),))],
+        compiler_params=pltpu.CompilerParams(vmem_limit_bytes=8 * 1024 * 1024),
+    )(*values)
+
+
 def tiled(value, rows):
     lead = value.shape[:-2]
     tall, columns = value.shape[-2:]
@@ -419,7 +470,7 @@
     blocks = master_params.shape[0]
     states = [tiled(value, 2)[:, 0] for value in (master_params, first_moment, second_moment)]
     outs = fused(experts, blocks, step_offsets[None], block_map, tiled(delta[0], 8), *states)
-    return tuple(untiled(value) for value in outs)
+    return tuple(untiled(value) for value in stored(*outs))
 
 
 def solution(mesh):

time: 54.4 us -> 51.7 us (0.950)
  local copies, waits for them, and re-layouts: 2.77 us -> 0 us
    unnamed x3 -> x0, local copies, waits for them, and re-layouts: 2.77 us -> none
    pallas_call x0 -> x1, Pallas kernels: none -> 1.56 us  [stored(): pl.pallas_call(store, name='store', out_shape=tuple((jax.ShapeDtypeStruct...]
    pallas_call x1, Pallas kernels: 50.9 us -> 49.4 us  [fused(): pl.pallas_call(lambda *refs: kernel(experts, blocks, refs), name='outer_s...]
where the time goes in v3:
time: 51.7 us; the launch traced here: 51.6 us
  Pallas kernels  50.9 us (98%)
  between operations  0.64 us (1%)
    pallas_call x1, Pallas kernels, fused(): pl.pallas_call(lambda *refs: kernel(experts, blocks, refs), name='outer_s...  49.4 us
    pallas_call x1, Pallas kernels, stored(): pl.pallas_call(store, name='store', out_shape=tuple((jax.ShapeDtypeStruct...  1.56 us

profile of v3, /device:TPU:1, one launch (start us, length us, event | category | flops | bytes accessed | tf_op | source)
XLA Modules:
  0.0 51.6 jit_solution(6060147388429541648)
XLA Ops:
  0.6 49.4 %outer_step.1 = (bf16[16,224,128]{2,1,0:T(8,128)(2,1)S(1)}, f32[16,112,128]{2,1,0:T(8,128)S(1)}, f32[16,112,128]{2,1,0:T(8,128)S(1)}) custom-call(s32[1,8]{1,0:T(1,128)} %bitcast.40, s32[256]{0:T(256)} %refs_1_.1, bf16[16,2,448,128]{3,2,1,0:T(8,128)(2,1)} %bitcast.36, f32[16,112,128]{2,1,0:T(8,128)} %bitcast.37, f32[16,112,128]{2,1,0:T(8,128)} %bitcast.38, ...), custom_call_target="tpu_custom_call" | custom-call | tf_op jit(solution)/shard_map/outer_step/pallas_call | solution.py:417
  50.0 1.6 %store.1 = (bf16[16,224,128]{2,1,0:T(8,128)(2,1)}, f32[16,112,128]{2,1,0:T(8,128)}, f32[16,112,128]{2,1,0:T(8,128)}) custom-call(bf16[16,224,128]{2,1,0:T(8,128)(2,1)S(1)} %get-tuple-element.9.refs_0_, f32[16,112,128]{2,1,0:T(8,128)S(1)} %get-tuple-element.10.refs_1_, f32[16,112,128]{2,1,0:T(8,128)S(1)} %get-tuple-element.11.refs_2_), custom_call_target="tpu_custom_call" | custom-call | tf_op jit(solution)/shard_map/store/pallas_call | solution.py:445

commit v4 on v3

--- a/solution.py
+++ b/solution.py
@@ -79,18 +79,6 @@
     device_x = {"replica": (1 - x) * RING + y}
     device_t = {"tensor": 1 - tensor}
 
-    barrier = pltpu.get_barrier_semaphore()
-    for device in (device_up, device_down, device_x, device_t):
-        pl.semaphore_signal(barrier, inc=1, device_id=device, device_id_type=MESH)
-
-    def greet(d, carry):
-        pl.semaphore_signal(
-            barrier, inc=1, device_id={"expert": (expert + d) % experts}, device_id_type=MESH
-        )
-        return carry
-
-    lax.fori_loop(1, experts, greet, 0)
-
     def load_delta(k):
         rows = pl.ds(starts[k] * TILES * 8, CHUNKS[k] * TILES * 8)
         return pltpu.make_async_copy(delta_ref.at[:, :, rows, :], delta_v[k], in_sem.at[k])
@@ -108,11 +96,24 @@
     load_offsets = pltpu.make_async_copy(offsets_hbm, offsets_ref, small_sem.at[1])
     load_map.start()
     load_offsets.start()
-    for k in range(chunks):
+    first_used = [int(number) for stage, number in ORDER if stage == "W"]
+    for k in first_used:
         load_delta(k).start()
     for k in range(chunks):
         for copy in load_states(k):
             copy.start()
+
+    barrier = pltpu.get_barrier_semaphore()
+    for device in (device_up, device_down, device_x, device_t):
+        pl.semaphore_signal(barrier, inc=1, device_id=device, device_id_type=MESH)
+
+    def greet(d, carry):
+        pl.semaphore_signal(
+            barrier, inc=1, device_id={"expert": (expert + d) % experts}, device_id_type=MESH
+        )
+        return carry
+
+    lax.fori_loop(1, experts, greet, 0)
 
     load_offsets.wait()
     reciprocal = 1.0 / (1.0 + offsets_ref[...].astype(F32))
@@ -299,14 +300,11 @@
         loop(step)
 
     def to_owners(k):
-        def send(i, carry):
+        for i in range(experts - 1):
             turn = i // 2
-            hops = (turn + 1) // 2 * (1 - 2 * (turn % 2))
-            z = (expert // 2 + experts // 4 + hops + experts) % (experts // 2)
+            hops = (turn + 1) // 2 * (1 - 2 * (turn % 2)) + experts // 4
+            z = (expert // 2 + hops) % (experts // 2)
             z_copy(k, 2 * z + (expert + 1 + i) % 2).start()
-            return carry
-
-        lax.fori_loop(0, experts - 1, send, 0)
         zrecv[k][expert] = zsend[k][expert]
 
     def all_of(k, ref, sem):
@@ -381,7 +379,9 @@
         for copy in far_copies(k) + pass_copies(k) + plain_copies(k) + [x_copy(k)]:
             copy.wait_send()
         all_of(k, zsend[k], z_send).wait()
-        t_copy(k).wait()
+    for stage, number in ORDER:
+        if stage == "U":
+            t_copy(int(number)).wait()
 
 
 def fused(experts, blocks, *operands):

time: 51.7 us -> 50.8 us (0.983)
  Pallas kernels: 50.9 us -> 50.1 us
    pallas_call x1, Pallas kernels: 49.4 us -> 48.6 us  [fused(): pl.pallas_call(lambda *refs: kernel(experts, blocks, refs), name='outer_s...]
where the time goes in v4:
time: 50.8 us
  Pallas kernels  50.1 us (99%)
  between operations  0.64 us (1%)
    pallas_call x1, Pallas kernels, fused(): pl.pallas_call(lambda *refs: kernel(experts, blocks, refs), name='outer_s...  48.6 us
    pallas_call x1, Pallas kernels, stored(): pl.pallas_call(store, name='store', out_shape=tuple((jax.ShapeDtypeStruct...  1.56 us

profile of v4, /device:TPU:1, one launch (start us, length us, event | category | flops | bytes accessed | tf_op | source)
XLA Modules:
  0.0 50.8 jit_solution(13328387082655808186)
XLA Ops:
  0.6 48.6 %outer_step.1 = (bf16[16,224,128]{2,1,0:T(8,128)(2,1)S(1)}, f32[16,112,128]{2,1,0:T(8,128)S(1)}, f32[16,112,128]{2,1,0:T(8,128)S(1)}) custom-call(s32[1,8]{1,0:T(1,128)} %bitcast.40, s32[256]{0:T(256)} %refs_1_.1, bf16[16,2,448,128]{3,2,1,0:T(8,128)(2,1)} %bitcast.36, f32[16,112,128]{2,1,0:T(8,128)} %bitcast.37, f32[16,112,128]{2,1,0:T(8,128)} %bitcast.38, ...), custom_call_target="tpu_custom_call" | custom-call | tf_op jit(solution)/shard_map/outer_step/pallas_call | solution.py:417
  49.2 1.6 %store.1 = (bf16[16,224,128]{2,1,0:T(8,128)(2,1)}, f32[16,112,128]{2,1,0:T(8,128)}, f32[16,112,128]{2,1,0:T(8,128)}) custom-call(bf16[16,224,128]{2,1,0:T(8,128)(2,1)S(1)} %get-tuple-element.9.refs_0_, f32[16,112,128]{2,1,0:T(8,128)S(1)} %get-tuple-element.10.refs_1_, f32[16,112,128]{2,1,0:T(8,128)S(1)} %get-tuple-element.11.refs_2_), custom_call_target="tpu_custom_call" | custom-call | tf_op jit(solution)/shard_map/store/pallas_call | solution.py:445

commit v5 on v4

--- a/solution.py
+++ b/solution.py
@@ -25,7 +25,7 @@
 LANES = 128
 TILES = 8
 RING = 4
-UNROLL = 4
+UNROLL = 8
 
 
 def adam(gradient, master, first, second):
@@ -434,7 +434,12 @@
 def store(*refs):
     count = len(refs) // 2
     sem = refs[-1]
-    copies = [pltpu.make_async_copy(refs[n], refs[count + n], sem.at[n]) for n in range(count)]
+    copies = []
+    for n in range(count):
+        part = refs[n].shape[0] // 4
+        for i in range(4):
+            rows = pl.ds(i * part, part)
+            copies.append(pltpu.make_async_copy(refs[n].at[rows], refs[count + n].at[rows], sem.at[4 * n + i]))
     for copy in copies:
         copy.start()
     for copy in copies:
@@ -448,7 +453,7 @@
         out_shape=tuple(jax.ShapeDtypeStruct(value.shape, value.dtype) for value in values),
         in_specs=[pl.BlockSpec(memory_space=pltpu.VMEM)] * len(values),
         out_specs=(pl.BlockSpec(memory_space=pltpu.HBM),) * len(values),
-        scratch_shapes=[pltpu.SemaphoreType.DMA((len(values),))],
+        scratch_shapes=[pltpu.SemaphoreType.DMA((4 * len(values),))],
         compiler_params=pltpu.CompilerParams(vmem_limit_bytes=8 * 1024 * 1024),
     )(*values)
 

time: 50.8 us -> 50.8 us (level)
  no operation moved by 1% of the time
where the time goes in v5:
time: 50.8 us
  Pallas kernels  50.1 us (99%)
  between operations  0.64 us (1%)
    pallas_call x1, Pallas kernels, fused(): pl.pallas_call(lambda *refs: kernel(experts, blocks, refs), name='outer_s...  48.5 us
    pallas_call x1, Pallas kernels, stored(): pl.pallas_call(store, name='store', out_shape=tuple((jax.ShapeDtypeStruct...  1.63 us

profile of v5, /device:TPU:1, one launch (start us, length us, event | category | flops | bytes accessed | tf_op | source)
XLA Modules:
  0.0 50.8 jit_solution(7778072112138589163)
XLA Ops:
  0.6 48.5 %outer_step.1 = (bf16[16,224,128]{2,1,0:T(8,128)(2,1)S(1)}, f32[16,112,128]{2,1,0:T(8,128)S(1)}, f32[16,112,128]{2,1,0:T(8,128)S(1)}) custom-call(s32[1,8]{1,0:T(1,128)} %bitcast.40, s32[256]{0:T(256)} %refs_1_.1, bf16[16,2,448,128]{3,2,1,0:T(8,128)(2,1)} %bitcast.36, f32[16,112,128]{2,1,0:T(8,128)} %bitcast.37, f32[16,112,128]{2,1,0:T(8,128)} %bitcast.38, ...), custom_call_target="tpu_custom_call" | custom-call | tf_op jit(solution)/shard_map/outer_step/pallas_call | solution.py:417
  49.1 1.6 %store.1 = (bf16[16,224,128]{2,1,0:T(8,128)(2,1)}, f32[16,112,128]{2,1,0:T(8,128)}, f32[16,112,128]{2,1,0:T(8,128)}) custom-call(bf16[16,224,128]{2,1,0:T(8,128)(2,1)S(1)} %get-tuple-element.9.refs_0_, f32[16,112,128]{2,1,0:T(8,128)S(1)} %get-tuple-element.10.refs_1_, f32[16,112,128]{2,1,0:T(8,128)S(1)} %get-tuple-element.11.refs_2_), custom_call_target="tpu_custom_call" | custom-call | tf_op jit(solution)/shard_map/store/pallas_call | solution.py:450
